TPU v7x, 768 devices: a whole 4x8x12 slice. The times are simulated.
768 devices in a mesh: tok: 12 (over x, z_lo), row: 2 (over core), col: 32 (over z_hi, y).
Axes of the slice: x: 4, y: 8, z: 12 (z_hi: 4, z_lo: 3; z = z_hi * 3 + z_lo), core: 2. Of those that a mesh axis runs over, the one named last changes fastest.
Arguments:
- activations: bfloat16 [6144, 4096], P(('tok', 'col'), 'row'), may hold values from -6 to 6
- grads_t: bfloat16 [12, 2464, 6144], P(None, 'col', ('tok', 'row')), may hold values from -0.14941406 to 0.14941406
Outputs:
- weight_grad: float32 [12, 2464, 4096], P('tok', 'col', 'row')
All inputs are finite; a program needn't handle non-finite values.
Results may differ from a plain program's by a relative error of at most 0.0003.
Values may be sent and summed in bfloat16 or wider, within the bound.
No kernel may reach another device: no remote copies, remote signals or barrier semaphores. Data moves between devices by JAX's collectives and lax.ppermute only.
A program may use at most 32 MiB of HBM per device.

v0:
```python
import jax
import jax.numpy as jnp
from jax import lax
from jax.sharding import Mesh
from jax.sharding import PartitionSpec as P

COL = ("col_0", "col_1")
TOK = ("tok_0", "tok_1")
TOK_COL = ("tok_0", "tok_1", "col_0", "col_1")
TOK_ROW = ("tok_0", "tok_1", "row")


def from_everyone(array, axis):
    count = lax.axis_size(axis)
    return lax.all_to_all(
        jnp.broadcast_to(array[None], (count, *array.shape)), axis, 0, 0, tiled=True
    )


def laid_out(blocks, dim):
    blocks = jnp.moveaxis(blocks, 0, dim)
    shape = blocks.shape
    return blocks.reshape(*shape[:dim], shape[dim] * shape[dim + 1], *shape[dim + 2 :])


def gather_directly(array, axis, dim):
    blocks = from_everyone(array, axis)
    return laid_out(blocks, dim)


def all_blocks(array, axes, order):
    blocks = array[None]
    for k in order:
        blocks = lax.all_gather(blocks, axes[k], axis=0, tiled=True)
    held = [lax.axis_size(axes[k]) for k in reversed(order)]
    blocks = blocks.reshape(*held, *array.shape)
    turned = sorted(range(len(order)), key=lambda place: order[len(order) - 1 - place])
    return blocks.transpose(*turned, *range(len(order), blocks.ndim)).reshape(-1, *array.shape)


def gather_axes(array, axes, order, dim):
    return laid_out(all_blocks(array, axes, order), dim)


def scatter_axes(array, axes, dim):
    if not axes:
        return array
    nearer = lax.psum_scatter(array, axes[0], scatter_dimension=dim, tiled=True)
    return scatter_axes(nearer, axes[1:], dim)


def body(activations, grads_t):
    groups, units, own = grads_t.shape
    grads_all = gather_directly(grads_t, "row", 2)
    acts_all = gather_axes(activations, COL, (0, 1), 0)
    width = acts_all.shape[1]
    flat = grads_all.reshape(groups * units, grads_all.shape[2])
    tile = jnp.dot(flat, acts_all, preferred_element_type=jnp.float32)
    result = scatter_axes(tile.reshape(groups, units, width), TOK, 0)
    return result


def solution(mesh):
    finer = Mesh(
        mesh.devices.reshape(4, 3, mesh.shape["row"], 4, 8),
        ("tok_0", "tok_1", "row", "col_0", "col_1"),
    )
    in_specs = (P(TOK_COL, "row"), P(None, COL, TOK_ROW))
    out_specs = P(TOK, COL, "row")
    return jax.shard_map(body, mesh=finer, in_specs=in_specs, out_specs=out_specs, check_vma=False)
```

profile of v0, /device:TPU:1, one launch (start us, length us, event | category | flops | bytes accessed | tf_op | source)
XLA Modules:
  0.0 229.6 jit_solution(14423356667424886688)
XLA Ops:
  6.5 0.0 all-gather.3.cloned.1.call-start
  6.5 24.6 %all-gather = bf16[64,2048]{1,0:T(8,128)(2,1)} all-gather(bf16[16,2048]{1,0:T(8,128)(2,1)} %param.2), channel_id=2, replica_groups=mesh['tok_0'=4,'tok_1'=3,'row'=2,'col_0'=4,'col_1'=8] {'col_0'}, dimensions={0}, use_global_device_ids=true | all-gather | bytes 327680 | tf_op jit(solution)/shard_map/all_gather | solution.py:34
  31.2 0.0 all-gather.3.cloned.1.call-update
  31.2 0.0 reduce-scatter.3.cloned.1.call-start
  31.3 1.1 broadcast_in_dim.4
  32.4 7.5 %all_to_all.5 = bf16[2,12,77,256]{3,2,1,0:T(8,128)(2,1)S(1)} all-to-all(bf16[2,12,77,256]{3,2,1,0:T(8,128)(2,1)S(1)} %broadcast_in_dim.4), channel_id=1, replica_groups=mesh['tok_0'=4,'tok_1'=3,'row'=2,'col_0'=4,'col_1'=8] {'row'}, dimensions={0} | all-to-all | bytes 1892352 | tf_op jit(solution)/shard_map/all_to_all | solution.py:15
  39.9 1.0 copy.6
  40.9 0.6 dot_general.5
  41.5 33.4 %all-gather.3.cloned.1.call-done = bf16[32,16,2048]{2,1,0:T(8,128)(2,1)} async-done(((bf16[4,16,2048]{2,1,0:T(8,128)(2,1)}), bf16[32,16,2048]{2,1,0:T(8,128)(2,1)}) %all-gather.3.cloned.1.call-update) | async-done | bytes 2097168 | tf_op jit(solution)/shard_map/all_gather | solution.py:34
  74.8 1.7 copy.7
  76.6 5.3 %fusion = f32[12,77,2048]{2,1,0:T(8,128)} fusion(bf16[12,77,512]{2,1,0:T(8,128)(2,1)S(1)} %dot_general.5, bf16[512,2048,1]{1,0,2:T(8,128)(2,1)S(1)} %bitcast.12), kind=kOutput, calls=%fused_computation | convolution fusion | flops 1937768448 | bytes 10612736 | tf_op jit(solution)/shard_map/dot_general | solution.py:58
  81.9 0.0 reduce-scatter.3.cloned.1.call-update
  81.9 0.0 reduce-scatter.5.cloned.1.call-start
  81.9 87.9 %reduce-scatter.3.cloned.1.call-done = f32[3,77,2048]{2,1,0:T(8,128)} async-done(((f32[12,77,2048]{2,1,0:T(8,128)}), f32[3,77,2048]{2,1,0:T(8,128)}) %reduce-scatter.3.cloned.1.call-update) | async-done | bytes 1892368 | tf_op jit(solution)/shard_map/reduce_scatter | solution.py:48
  169.8 0.0 reduce-scatter.5.cloned.1.call-update
  169.8 50.7 %reduce-scatter.5.cloned.1.call-done = f32[1,77,2048]{2,1,0:T(8,128)} async-done(((f32[3,77,2048]{2,1,0:T(8,128)}), f32[1,77,2048]{2,1,0:T(8,128)}) %reduce-scatter.5.cloned.1.call-update) | async-done | bytes 630800 | tf_op jit(solution)/shard_map/reduce_scatter | solution.py:48
  220.5 2.6 %copy.8 = f32[1,77,2048]{2,0,1:T(1,128)} copy(f32[1,77,2048]{2,1,0:T(8,128)} %reduce-scatter.5.cloned.1.call-done) | data formatting | bytes 1261568 | tf_op jit(solution)/shard_map/reduce_scatter | solution.py:48
Async XLA Ops:
  6.5 68.3 %all-gather.3.cloned.1.call-start = ((), (), s32[]{:S(2)}) async-start(), calls=%async_computation.3 | async-start | bytes 2359296 | tf_op jit(solution)/shard_map/all_gather | solution.py:34
  31.2 138.6 %reduce-scatter.3.cloned.1.call-start = ((), (), s32[]{:S(2)}) async-start(), calls=%async_computation.4 | async-start | bytes 9830400 | tf_op jit(solution)/shard_map/reduce_scatter | solution.py:48
  81.9 138.6 %reduce-scatter.5.cloned.1.call-start = ((), (), s32[]{:S(2)}) async-start(), calls=%async_computation.5 | async-start | bytes 2621440 | tf_op jit(solution)/shard_map/reduce_scatter | solution.py:48
Sparse Core Ops, SparseCore 0:
  31.3 43.4 all-gather.2
  82.0 87.7 reduce-scatter.2
  173.0 47.5 reduce-scatter.4
where the time goes:
time: 230 us
  waiting for transfers between devices  172 us (75%)
  blocking collectives  32.2 us (14%)
  between operations  13.1 us (6%)
  local copies, waits for them, and re-layouts  6.97 us (3%)
  matrix products  5.28 us (2%)
    reduce_scatter x2, waiting for transfers between devices, scatter_axes(): nearer = lax.psum_scatter(array, axes[0], scatter_dimension=dim, tiled=True)  139 us
    all_gather x1, waiting for transfers between devices, all_blocks(): blocks = lax.all_gather(blocks, axes[k], axis=0, tiled=True)  33.4 us
    all_gather x1, blocking collectives, all_blocks(): blocks = lax.all_gather(blocks, axes[k], axis=0, tiled=True)  24.6 us
    all_to_all x1, blocking collectives, from_everyone(): lax.all_to_all(jnp.broadcast_to(array[None], (count, *array.shape)), axis...  7.53 us
    dot_general x1, matrix products, body(): tile = jnp.dot(flat, acts_all, preferred_element_type=jnp.float32)  5.28 us
  transfers between devices with their start and end apart: 3, of which 3 were waited for; matrix products, arithmetic and copies ran while one was open for 1% of the time, Pallas kernels for 0%

commit v1 on v0

v1 whole, which is shorter than its diff:
```python
import jax
import jax.numpy as jnp
from jax import lax
from jax.experimental import pallas as pl
from jax.experimental.pallas import tpu as pltpu
from jax.sharding import Mesh
from jax.sharding import PartitionSpec as P


TOK = ("tok_0", "tok_1")


def exchange(blocks, axis):
    return lax.all_to_all(blocks, axis, 0, 0, tiled=True)


def shifted(array, axis, by):
    count = lax.axis_size(axis)
    return lax.ppermute(array, axis, [(k, (k + by) % count) for k in range(count)])


def round_the_ring(piece):
    count, place = lax.axis_size("col_1"), lax.axis_index("col_1")
    outer, own, width = piece.shape
    rows = jnp.zeros((outer, count, own, width), piece.dtype)

    def put(rows, block, source):
        return lax.dynamic_update_slice(rows, block[:, None], (0, source % count, 0, 0))

    rows = put(rows, piece, place)
    up = down = piece
    for step in range(1, count // 2):
        up, down = shifted(up, "col_1", 1), shifted(down, "col_1", -1)
        rows = put(put(rows, up, place - step + count), down, place + step)
    half = outer // 2
    last = jnp.concatenate([shifted(up[:half], "col_1", 1), shifted(down[half:], "col_1", -1)])
    rows = put(rows, last, place + count // 2)
    return rows.reshape(-1, width)


def product_kernel(side_ref, mine_ref, other_ref, rows_ref, out_ref, total_ref, *, units):
    blocks, _, depth = mine_ref.shape
    side = side_ref[0]
    for k in range(blocks):
        own = rows_ref[pl.ds(pl.multiple_of((2 * k + side) * depth, depth), depth), :]
        far = rows_ref[pl.ds(pl.multiple_of((2 * k + 1 - side) * depth, depth), depth), :]
        add = jnp.dot(mine_ref[k], own, preferred_element_type=jnp.float32)
        add += jnp.dot(other_ref[k], far, preferred_element_type=jnp.float32)
        if k == 0:
            total_ref[...] = add
        else:
            total_ref[...] += add
    limit = jnp.maximum(jnp.max(jnp.abs(total_ref[...])), 1e-30)
    exponent = jnp.ceil(jnp.log2(jnp.full((1, 128), limit, jnp.float32))) - 15.0
    exponent = jnp.max(exponent)
    scale = jnp.max(jnp.exp2(jnp.full((1, 128), -exponent, jnp.float32)))
    groups, padded, _ = out_ref.shape
    row = lax.broadcasted_iota(jnp.int32, out_ref.shape[1:], 0)
    for g in range(groups):
        values = total_ref[g * padded : (g + 1) * padded, :] * scale
        out_ref[g] = jnp.where(row < units, values, exponent)


def product(side, mine, other, rows, groups, units):
    _, height, _ = mine.shape
    width = rows.shape[1]
    return pl.pallas_call(
        lambda *refs: product_kernel(*refs, units=units),
        out_shape=jax.ShapeDtypeStruct((groups, height // groups, width), jnp.float32),
        in_specs=[
            pl.BlockSpec(memory_space=pltpu.SMEM),
            *(pl.BlockSpec(memory_space=pltpu.VMEM) for _ in range(3)),
        ],
        out_specs=pl.BlockSpec(memory_space=pltpu.VMEM),
        scratch_shapes=[pltpu.VMEM((height, width), jnp.float32)],
        compiler_params=pltpu.CompilerParams(vmem_limit_bytes=24 * 1024 * 1024),
        name="product",
    )(side, mine, other, rows)


def body(activations, grads_t):
    across, lower, outer = (lax.axis_size(name) for name in ("tok_0", "tok_1", "col_0"))
    groups, units, part = grads_t.shape
    own, width = activations.shape
    quarter = width // across
    padded = -(-units // 8) * 8 if units % 8 else units + 8

    quarters = activations.reshape(own, across, quarter).transpose(1, 0, 2)
    sent = jnp.broadcast_to(quarters[:, None], (across, outer, own, quarter)).reshape(-1, own, quarter)
    near = exchange(sent, ("tok_0", "col_0"))
    rows = round_the_ring(near)

    flat = jnp.pad(grads_t, ((0, 0), (0, padded - units), (0, 0))).reshape(groups * padded, part)
    mine = exchange(jnp.broadcast_to(flat[None], (across, *flat.shape)), "tok_0")
    other = shifted(mine, "row", 1)
    side = lax.axis_index("row").astype(jnp.int32)[None]
    partial = product(side, mine, other, rows, groups, units)
    received = exchange(partial.astype(jnp.float16), TOK)
    received = received.reshape(across, lower, padded, quarter)
    scale = jnp.exp2(received[:, :, units : units + 1, :1].astype(jnp.float32))
    sums = jnp.sum(received[:, :, :units].astype(jnp.float32) * scale, axis=1)
    return jnp.concatenate([sums[k] for k in range(across)], axis=-1)[None]


def solution(mesh):
    finer = Mesh(
        mesh.devices.reshape(4, 3, mesh.shape["row"], 4, 8),
        ("tok_0", "tok_1", "row", "col_0", "col_1"),
    )
    col, tok_col, tok_row = ("col_0", "col_1"), (*TOK, "col_0", "col_1"), (*TOK, "row")
    in_specs = (P(tok_col, "row"), P(None, col, tok_row))
    out_specs = P(TOK, col, "row")
    return jax.shard_map(body, mesh=finer, in_specs=in_specs, out_specs=out_specs, check_vma=False)
```

time: 230 us -> 133 us (0.58)
  the two profiles are of different devices: /device:TPU:1 before, /device:TPU:24 now
where the time goes in v1:
time: 133 us; the launch traced here: 132 us
  starting transfers between devices  50.7 us (38%)
  waiting for transfers between devices  50.3 us (38%)
  blocking collectives  20.8 us (16%)
  local copies, waits for them, and re-layouts  5.15 us (4%)
  Pallas kernels  4.07 us (3%)
    all_to_all x2, waiting for transfers between devices, exchange(): return lax.all_to_all(blocks, axis, 0, 0, tiled=True)  37.4 us
    ppermute x9, starting transfers between devices, shifted(): lax.ppermute(array, axis, [(k, (k + by) % count) for k in range(count)])  31.1 us
    all_to_all x1, blocking collectives, exchange(): return lax.all_to_all(blocks, axis, 0, 0, tiled=True)  20.8 us
    all_to_all x2, starting transfers between devices, exchange(): return lax.all_to_all(blocks, axis, 0, 0, tiled=True)  19.6 us
    ppermute x9, waiting for transfers between devices, shifted(): lax.ppermute(array, axis, [(k, (k + by) % count) for k in range(count)])  12.9 us
    pallas_call x1, Pallas kernels, product(): pl.pallas_call(lambda *refs: product_kernel(*refs, units=units), out_shap...  4.07 us
  transfers between devices with their start and end apart: 11, of which 8 were waited for; matrix products, arithmetic and copies ran while one was open for 0% of the time, Pallas kernels for 0%

profile of v1, /device:TPU:24, one launch (start us, length us, event | category | flops | bytes accessed | tf_op | source)
XLA Modules:
  0.0 132.0 jit_solution(15159392758630299088)
XLA Ops:
  0.0 1.1 pad.4
  1.1 1.4 %broadcast_in_dim.48 = bf16[4,960,256]{2,1,0:T(8,128)(2,1)} broadcast(bf16[960,256]{1,0:T(8,128)(2,1)S(1)} %bitcast.51), dimensions={1,2} | broadcast | bytes 2457600 | tf_op jit(solution)/shard_map/broadcast_in_dim | solution.py:94
  2.5 4.4 %all-to-all-start = ((bf16[4,960,256]{2,1,0:T(8,128)(2,1)}), bf16[4,960,256]{2,1,0:T(8,128)(2,1)S(1)}, u32[]{:S(2)}, u32[]{:S(2)}) async-start(bf16[4,960,256]{2,1,0:T(8,128)(2,1)} %broadcast_in_dim.48), calls=%async_computation | async-start | bytes 3932160 | tf_op jit(solution)/shard_map/all_to_all | solution.py:14
  7.0 24.9 %all-to-all-done.refs_1_ = bf16[4,960,256]{2,1,0:T(8,128)(2,1)S(1)} async-done(((bf16[4,960,256]{2,1,0:T(8,128)(2,1)}), bf16[4,960,256]{2,1,0:T(8,128)(2,1)S(1)}, u32[]{:S(2)}, u32[]{:S(2)}) %all-to-all-start) | async-done | bytes 1966112 | tf_op jit(solution)/shard_map/all_to_all | solution.py:14
  31.8 0.7 broadcast_in_dim.50
  32.6 15.2 %all-to-all-start.1 = ((bf16[16,16,512]{2,1,0:T(8,128)(2,1)}), bf16[16,16,512]{2,1,0:T(8,128)(2,1)S(1)}, u32[]{:S(2)}, u32[]{:S(2)}) async-start(bf16[16,16,512]{2,1,0:T(8,128)(2,1)} %bitcast.3), calls=%async_computation.1 | async-start | bytes 524288 | tf_op jit(solution)/shard_map/all_to_all | solution.py:14
  47.8 1.9 %collective-permute-start = (bf16[4,960,256]{2,1,0:T(8,128)(2,1)S(1)}, bf16[4,960,256]{2,1,0:T(8,128)(2,1)}, u32[]{:S(2)}, u32[]{:S(2)}) collective-permute-start(bf16[4,960,256]{2,1,0:T(8,128)(2,1)S(1)} %all-to-all-done.refs_1_), channel_id=1, source_target_pairs={{0,32},{32,0},{1,33},{33,1},{2,34},{34,2},{3,35},{35,3},{4,36},{36... | collective-permute-start | bytes 5898248 | tf_op jit(solution)/shard_map/ppermute | solution.py:19
  49.7 12.5 %all-to-all-done.1 = bf16[16,16,512]{2,1,0:T(8,128)(2,1)S(1)} async-done(((bf16[16,16,512]{2,1,0:T(8,128)(2,1)}), bf16[16,16,512]{2,1,0:T(8,128)(2,1)S(1)}, u32[]{:S(2)}, u32[]{:S(2)}) %all-to-all-start.1) | async-done | bytes 262176 | tf_op jit(solution)/shard_map/all_to_all | solution.py:14
  62.2 4.7 %collective-permute-start.1 = (bf16[16,16,512]{2,1,0:T(8,128)(2,1)S(1)}, bf16[16,16,512]{2,1,0:T(8,128)(2,1)S(1)}, u32[]{:S(2)}, u32[]{:S(2)}) collective-permute-start(bf16[16,16,512]{2,1,0:T(8,128)(2,1)S(1)} %all-to-all-done.1), channel_id=1, source_target_pairs={{0,1},{1,2},{2,3},{3,4},{4,5},{5,6},{6,7},{7,0},{8,9},{9,10},{10,1... | collective-permute-start | bytes 786440 | tf_op jit(solution)/shard_map/ppermute | solution.py:19
  66.9 1.9 %collective-permute-start.2 = (bf16[16,16,512]{2,1,0:T(8,128)(2,1)S(1)}, bf16[16,16,512]{2,1,0:T(8,128)(2,1)S(1)}, u32[]{:S(2)}, u32[]{:S(2)}) collective-permute-start(bf16[16,16,512]{2,1,0:T(8,128)(2,1)S(1)} %all-to-all-done.1), channel_id=1, source_target_pairs={{0,7},{1,0},{2,1},{3,2},{4,3},{5,4},{6,5},{7,6},{8,15},{9,8},{10,9... | collective-permute-start | bytes 786440 | tf_op jit(solution)/shard_map/ppermute | solution.py:19
  68.9 0.3 broadcast_in_dim.49
  69.2 1.5 %collective-permute-done.1 = bf16[16,16,512]{2,1,0:T(8,128)(2,1)S(1)} collective-permute-done((bf16[16,16,512]{2,1,0:T(8,128)(2,1)S(1)}, bf16[16,16,512]{2,1,0:T(8,128)(2,1)S(1)}, u32[]{:S(2)}, u32[]{:S(2)}) %collective-permute-start.1) | collective-permute-done | bytes 262176 | tf_op jit(solution)/shard_map/ppermute | solution.py:19
  70.8 5.6 %collective-permute-start.3 = (bf16[16,16,512]{2,1,0:T(8,128)(2,1)S(1)}, bf16[16,16,512]{2,1,0:T(8,128)(2,1)S(1)}, u32[]{:S(2)}, u32[]{:S(2)}) collective-permute-start(bf16[16,16,512]{2,1,0:T(8,128)(2,1)S(1)} %collective-permute-done.1), channel_id=1, source_target_pairs={{0,1},{1,2},{2,3},{3,4},{4,5},{5,6},{6,7},{7,0},{8,9},{9,10},{10,1... | collective-permute-start | bytes 786440 | tf_op jit(solution)/shard_map/ppermute | solution.py:19
  76.4 0.0 collective-permute-done.2
  76.4 1.9 %collective-permute-start.4 = (bf16[16,16,512]{2,1,0:T(8,128)(2,1)S(1)}, bf16[16,16,512]{2,1,0:T(8,128)(2,1)S(1)}, u32[]{:S(2)}, u32[]{:S(2)}) collective-permute-start(bf16[16,16,512]{2,1,0:T(8,128)(2,1)S(1)} %collective-permute-done.2), channel_id=1, source_target_pairs={{0,7},{1,0},{2,1},{3,2},{4,3},{5,4},{6,5},{7,6},{8,15},{9,8},{10,9... | collective-permute-start | bytes 786440 | tf_op jit(solution)/shard_map/ppermute | solution.py:19
  78.4 1.9 %collective-permute-done.3 = bf16[16,16,512]{2,1,0:T(8,128)(2,1)S(1)} collective-permute-done((bf16[16,16,512]{2,1,0:T(8,128)(2,1)S(1)}, bf16[16,16,512]{2,1,0:T(8,128)(2,1)S(1)}, u32[]{:S(2)}, u32[]{:S(2)}) %collective-permute-start.3) | collective-permute-done | bytes 262176 | tf_op jit(solution)/shard_map/ppermute | solution.py:19
  80.2 5.6 %collective-permute-start.5 = (bf16[16,16,512]{2,1,0:T(8,128)(2,1)S(1)}, bf16[16,16,512]{2,1,0:T(8,128)(2,1)S(1)}, u32[]{:S(2)}, u32[]{:S(2)}) collective-permute-start(bf16[16,16,512]{2,1,0:T(8,128)(2,1)S(1)} %collective-permute-done.3), channel_id=1, source_target_pairs={{0,1},{1,2},{2,3},{3,4},{4,5},{5,6},{6,7},{7,0},{8,9},{9,10},{10,1... | collective-permute-start | bytes 786440 | tf_op jit(solution)/shard_map/ppermute | solution.py:19
  85.8 0.2 collective-permute-done.4
  86.1 1.9 %collective-permute-start.6 = (bf16[16,16,512]{2,1,0:T(8,128)(2,1)S(1)}, bf16[16,16,512]{2,1,0:T(8,128)(2,1)S(1)}, u32[]{:S(2)}, u32[]{:S(2)}) collective-permute-start(bf16[16,16,512]{2,1,0:T(8,128)(2,1)S(1)} %collective-permute-done.4), channel_id=1, source_target_pairs={{0,7},{1,0},{2,1},{3,2},{4,3},{5,4},{6,5},{7,6},{8,15},{9,8},{10,9... | collective-permute-start | bytes 786440 | tf_op jit(solution)/shard_map/ppermute | solution.py:19
  88.0 2.7 %collective-permute-done.5 = bf16[16,16,512]{2,1,0:T(8,128)(2,1)S(1)} collective-permute-done((bf16[16,16,512]{2,1,0:T(8,128)(2,1)S(1)}, bf16[16,16,512]{2,1,0:T(8,128)(2,1)S(1)}, u32[]{:S(2)}, u32[]{:S(2)}) %collective-permute-start.5) | collective-permute-done | bytes 262176 | tf_op jit(solution)/shard_map/ppermute | solution.py:19
  90.8 5.6 %collective-permute-start.7 = (bf16[8,16,512]{2,1,0:T(8,128)(2,1)S(1)}, bf16[8,16,512]{2,1,0:T(8,128)(2,1)S(1)}, u32[]{:S(2)}, u32[]{:S(2)}) collective-permute-start(bf16[8,16,512]{2,1,0:T(8,128)(2,1)S(1)} %slice.32), channel_id=1, source_target_pairs={{0,1},{1,2},{2,3},{3,4},{4,5},{5,6},{6,7},{7,0},{8,9},{9,10},{10,1... | collective-permute-start | bytes 393224 | tf_op jit(solution)/shard_map/ppermute | solution.py:19
  96.4 0.5 collective-permute-done.6
  96.9 1.9 %collective-permute-start.8 = (bf16[8,16,512]{2,1,0:T(8,128)(2,1)S(1)}, bf16[8,16,512]{2,1,0:T(8,128)(2,1)S(1)}, u32[]{:S(2)}, u32[]{:S(2)}) collective-permute-start(bf16[8,16,512]{2,1,0:T(8,128)(2,1)S(1)} %slice.33), channel_id=1, source_target_pairs={{0,7},{1,0},{2,1},{3,2},{4,3},{5,4},{6,5},{7,6},{8,15},{9,8},{10,9... | collective-permute-start | bytes 393224 | tf_op jit(solution)/shard_map/ppermute | solution.py:19
  98.9 0.0 collective-permute-done.7
  98.9 6.1 %collective-permute-done.8 = bf16[8,16,512]{2,1,0:T(8,128)(2,1)S(1)} collective-permute-done((bf16[8,16,512]{2,1,0:T(8,128)(2,1)S(1)}, bf16[8,16,512]{2,1,0:T(8,128)(2,1)S(1)}, u32[]{:S(2)}, u32[]{:S(2)}) %collective-permute-start.8) | collective-permute-done | bytes 131104 | tf_op jit(solution)/shard_map/ppermute | solution.py:19
  105.0 0.0 collective-permute-done.refs_2_
  105.0 4.1 %product.1 = f32[12,80,512]{2,1,0:T(8,128)S(1)} custom-call(s32[1]{0:T(128)} %bitcast.refs_0_, bf16[4,960,256]{2,1,0:T(8,128)(2,1)S(1)} %all-to-all-done.refs_1_, bf16[4,960,256]{2,1,0:T(8,128)(2,1)} %collective-permute-done.refs_2_, bf16[2048,512]{1,0:T(8,128)(2,1)S(1)} %bitcast.48), custom_call_target="tpu_custom_call" | custom-call | tf_op jit(solution)/shard_map/product/pallas_call | solution.py:67
  109.1 0.2 convert_element_type.11
  109.3 20.8 %all_to_all.15 = f16[12,80,512]{2,1,0:T(8,128)(2,1)S(1)} all-to-all(f16[12,80,512]{2,1,0:T(8,128)(2,1)S(1)} %convert_element_type.11), channel_id=1, replica_groups=mesh['tok_0'=4,'tok_1'=3,'row'=2,'col_0'=4,'col_1'=8] {'tok_0','tok_1'}, dimensions={0} | all-to-all | bytes 1966080 | tf_op jit(solution)/shard_map/all_to_all | solution.py:14
  130.1 0.1 copy.12
  130.3 0.3 multiply_reduce_fusion
  130.7 1.3 broadcast_in_dim.59
  (18 shorter events, 0.4 us)
Async XLA Ops:
  2.5 4.4 %copy-start = (bf16[16,2048]{1,0:T(8,128)(2,1)S(1)}, bf16[16,2048]{1,0:T(8,128)(2,1)}, u32[]{:S(2)}) copy-start(bf16[16,2048]{1,0:T(8,128)(2,1)} %param.2) | copy-start | bytes 196612
  2.5 29.4 %all-to-all-start = ((bf16[4,960,256]{2,1,0:T(8,128)(2,1)}), bf16[4,960,256]{2,1,0:T(8,128)(2,1)S(1)}, u32[]{:S(2)}, u32[]{:S(2)}) async-start(bf16[4,960,256]{2,1,0:T(8,128)(2,1)} %broadcast_in_dim.48), calls=%async_computation | async-start | bytes 3932160 | tf_op jit(solution)/shard_map/all_to_all | solution.py:14
  32.6 29.6 %all-to-all-start.1 = ((bf16[16,16,512]{2,1,0:T(8,128)(2,1)}), bf16[16,16,512]{2,1,0:T(8,128)(2,1)S(1)}, u32[]{:S(2)}, u32[]{:S(2)}) async-start(bf16[16,16,512]{2,1,0:T(8,128)(2,1)} %bitcast.3), calls=%async_computation.1 | async-start | bytes 524288 | tf_op jit(solution)/shard_map/all_to_all | solution.py:14
  47.8 57.2 %collective-permute-start = (bf16[4,960,256]{2,1,0:T(8,128)(2,1)S(1)}, bf16[4,960,256]{2,1,0:T(8,128)(2,1)}, u32[]{:S(2)}, u32[]{:S(2)}) collective-permute-start(bf16[4,960,256]{2,1,0:T(8,128)(2,1)S(1)} %all-to-all-done.refs_1_), channel_id=1, source_target_pairs={{0,32},{32,0},{1,33},{33,1},{2,34},{34,2},{3,35},{35,3},{4,36},{36... | collective-permute-start | bytes 5898248 | tf_op jit(solution)/shard_map/ppermute | solution.py:19
  62.2 8.6 %collective-permute-start.1 = (bf16[16,16,512]{2,1,0:T(8,128)(2,1)S(1)}, bf16[16,16,512]{2,1,0:T(8,128)(2,1)S(1)}, u32[]{:S(2)}, u32[]{:S(2)}) collective-permute-start(bf16[16,16,512]{2,1,0:T(8,128)(2,1)S(1)} %all-to-all-done.1), channel_id=1, source_target_pairs={{0,1},{1,2},{2,3},{3,4},{4,5},{5,6},{6,7},{7,0},{8,9},{9,10},{10,1... | collective-permute-start | bytes 786440 | tf_op jit(solution)/shard_map/ppermute | solution.py:19
  66.9 9.5 %collective-permute-start.2 = (bf16[16,16,512]{2,1,0:T(8,128)(2,1)S(1)}, bf16[16,16,512]{2,1,0:T(8,128)(2,1)S(1)}, u32[]{:S(2)}, u32[]{:S(2)}) collective-permute-start(bf16[16,16,512]{2,1,0:T(8,128)(2,1)S(1)} %all-to-all-done.1), channel_id=1, source_target_pairs={{0,7},{1,0},{2,1},{3,2},{4,3},{5,4},{6,5},{7,6},{8,15},{9,8},{10,9... | collective-permute-start | bytes 786440 | tf_op jit(solution)/shard_map/ppermute | solution.py:19
  70.8 9.5 %collective-permute-start.3 = (bf16[16,16,512]{2,1,0:T(8,128)(2,1)S(1)}, bf16[16,16,512]{2,1,0:T(8,128)(2,1)S(1)}, u32[]{:S(2)}, u32[]{:S(2)}) collective-permute-start(bf16[16,16,512]{2,1,0:T(8,128)(2,1)S(1)} %collective-permute-done.1), channel_id=1, source_target_pairs={{0,1},{1,2},{2,3},{3,4},{4,5},{5,6},{6,7},{7,0},{8,9},{9,10},{10,1... | collective-permute-start | bytes 786440 | tf_op jit(solution)/shard_map/ppermute | solution.py:19
  76.4 9.7 %collective-permute-start.4 = (bf16[16,16,512]{2,1,0:T(8,128)(2,1)S(1)}, bf16[16,16,512]{2,1,0:T(8,128)(2,1)S(1)}, u32[]{:S(2)}, u32[]{:S(2)}) collective-permute-start(bf16[16,16,512]{2,1,0:T(8,128)(2,1)S(1)} %collective-permute-done.2), channel_id=1, source_target_pairs={{0,7},{1,0},{2,1},{3,2},{4,3},{5,4},{6,5},{7,6},{8,15},{9,8},{10,9... | collective-permute-start | bytes 786440 | tf_op jit(solution)/shard_map/ppermute | solution.py:19
  80.2 10.5 %collective-permute-start.5 = (bf16[16,16,512]{2,1,0:T(8,128)(2,1)S(1)}, bf16[16,16,512]{2,1,0:T(8,128)(2,1)S(1)}, u32[]{:S(2)}, u32[]{:S(2)}) collective-permute-start(bf16[16,16,512]{2,1,0:T(8,128)(2,1)S(1)} %collective-permute-done.3), channel_id=1, source_target_pairs={{0,1},{1,2},{2,3},{3,4},{4,5},{5,6},{6,7},{7,0},{8,9},{9,10},{10,1... | collective-permute-start | bytes 786440 | tf_op jit(solution)/shard_map/ppermute | solution.py:19
  86.1 10.8 %collective-permute-start.6 = (bf16[16,16,512]{2,1,0:T(8,128)(2,1)S(1)}, bf16[16,16,512]{2,1,0:T(8,128)(2,1)S(1)}, u32[]{:S(2)}, u32[]{:S(2)}) collective-permute-start(bf16[16,16,512]{2,1,0:T(8,128)(2,1)S(1)} %collective-permute-done.4), channel_id=1, source_target_pairs={{0,7},{1,0},{2,1},{3,2},{4,3},{5,4},{6,5},{7,6},{8,15},{9,8},{10,9... | collective-permute-start | bytes 786440 | tf_op jit(solution)/shard_map/ppermute | solution.py:19
  90.8 8.1 %collective-permute-start.7 = (bf16[8,16,512]{2,1,0:T(8,128)(2,1)S(1)}, bf16[8,16,512]{2,1,0:T(8,128)(2,1)S(1)}, u32[]{:S(2)}, u32[]{:S(2)}) collective-permute-start(bf16[8,16,512]{2,1,0:T(8,128)(2,1)S(1)} %slice.32), channel_id=1, source_target_pairs={{0,1},{1,2},{2,3},{3,4},{4,5},{5,6},{6,7},{7,0},{8,9},{9,10},{10,1... | collective-permute-start | bytes 393224 | tf_op jit(solution)/shard_map/ppermute | solution.py:19
  96.9 8.1 %collective-permute-start.8 = (bf16[8,16,512]{2,1,0:T(8,128)(2,1)S(1)}, bf16[8,16,512]{2,1,0:T(8,128)(2,1)S(1)}, u32[]{:S(2)}, u32[]{:S(2)}) collective-permute-start(bf16[8,16,512]{2,1,0:T(8,128)(2,1)S(1)} %slice.33), channel_id=1, source_target_pairs={{0,7},{1,0},{2,1},{3,2},{4,3},{5,4},{6,5},{7,6},{8,15},{9,8},{10,9... | collective-permute-start | bytes 393224 | tf_op jit(solution)/shard_map/ppermute | solution.py:19

commit v2 on v1

--- a/solution.py
+++ b/solution.py
@@ -19,31 +19,39 @@
     return lax.ppermute(array, axis, [(k, (k + by) % count) for k in range(count)])
 
 
+def passed_on(array, by):
+    count = lax.axis_size("col_1")
+    steps = [(k, (k + by) % count) for k in range(count)]
+    steps += [(count + k, count + (k - by) % count) for k in range(count)]
+    return lax.ppermute(array, ("row", "col_1"), steps)
+
+
 def round_the_ring(piece):
     count, place = lax.axis_size("col_1"), lax.axis_index("col_1")
+    way = 1 - 2 * lax.axis_index("row")
     outer, own, width = piece.shape
     rows = jnp.zeros((outer, count, own, width), piece.dtype)
 
     def put(rows, block, source):
-        return lax.dynamic_update_slice(rows, block[:, None], (0, source % count, 0, 0))
+        return lax.dynamic_update_slice(rows, block[:, None], (0, (source + count) % count, 0, 0))
 
     rows = put(rows, piece, place)
-    up = down = piece
-    for step in range(1, count // 2):
-        up, down = shifted(up, "col_1", 1), shifted(down, "col_1", -1)
-        rows = put(put(rows, up, place - step + count), down, place + step)
-    half = outer // 2
-    last = jnp.concatenate([shifted(up[:half], "col_1", 1), shifted(down[half:], "col_1", -1)])
-    rows = put(rows, last, place + count // 2)
+    ahead1, back1 = passed_on(piece, 1), passed_on(piece, -1)
+    ahead2, back2 = passed_on(piece, 2), passed_on(piece, -2)
+    ahead3, back3 = passed_on(ahead2, 1), passed_on(back2, -1)
+    ahead4 = passed_on(ahead2, 2)
+    for step, block in ((1, ahead1), (-1, back1), (2, ahead2), (-2, back2), (3, ahead3), (4, ahead4), (-3, back3)):
+        rows = put(rows, block, place - way * step)
     return rows.reshape(-1, width)
 
 
-def product_kernel(side_ref, mine_ref, other_ref, rows_ref, out_ref, total_ref, *, units):
+def product_kernel(place_ref, mine_ref, other_ref, rows_ref, out_ref, total_ref, *, units):
     blocks, _, depth = mine_ref.shape
-    side = side_ref[0]
+    side, across = place_ref[0], place_ref[1]
     for k in range(blocks):
-        own = rows_ref[pl.ds(pl.multiple_of((2 * k + side) * depth, depth), depth), :]
-        far = rows_ref[pl.ds(pl.multiple_of((2 * k + 1 - side) * depth, depth), depth), :]
+        first = 2 * lax.rem(across + blocks - k, blocks)
+        own = rows_ref[pl.ds(pl.multiple_of((first + side) * depth, depth), depth), :]
+        far = rows_ref[pl.ds(pl.multiple_of((first + 1 - side) * depth, depth), depth), :]
         add = jnp.dot(mine_ref[k], own, preferred_element_type=jnp.float32)
         add += jnp.dot(other_ref[k], far, preferred_element_type=jnp.float32)
         if k == 0:
@@ -61,7 +69,7 @@
         out_ref[g] = jnp.where(row < units, values, exponent)
 
 
-def product(side, mine, other, rows, groups, units):
+def product(place, mine, other, rows, groups, units):
     _, height, _ = mine.shape
     width = rows.shape[1]
     return pl.pallas_call(
@@ -75,26 +83,27 @@
         scratch_shapes=[pltpu.VMEM((height, width), jnp.float32)],
         compiler_params=pltpu.CompilerParams(vmem_limit_bytes=24 * 1024 * 1024),
         name="product",
-    )(side, mine, other, rows)
+    )(place, mine, other, rows)
 
 
 def body(activations, grads_t):
     across, lower, outer = (lax.axis_size(name) for name in ("tok_0", "tok_1", "col_0"))
-    groups, units, part = grads_t.shape
+    groups, units, held = grads_t.shape
     own, width = activations.shape
     quarter = width // across
     padded = -(-units // 8) * 8 if units % 8 else units + 8
 
-    quarters = activations.reshape(own, across, quarter).transpose(1, 0, 2)
+    quarters = jnp.stack([activations[:, k * quarter : (k + 1) * quarter] for k in range(across)])
     sent = jnp.broadcast_to(quarters[:, None], (across, outer, own, quarter)).reshape(-1, own, quarter)
     near = exchange(sent, ("tok_0", "col_0"))
     rows = round_the_ring(near)
 
-    flat = jnp.pad(grads_t, ((0, 0), (0, padded - units), (0, 0))).reshape(groups * padded, part)
-    mine = exchange(jnp.broadcast_to(flat[None], (across, *flat.shape)), "tok_0")
+    flat = jnp.pad(grads_t, ((0, 0), (0, padded - units), (0, 0))).reshape(groups * padded, held)
+    blocks = [flat, *(shifted(flat, "tok_0", k) for k in range(1, across))]
+    mine = jnp.stack(blocks)
     other = shifted(mine, "row", 1)
-    side = lax.axis_index("row").astype(jnp.int32)[None]
-    partial = product(side, mine, other, rows, groups, units)
+    place = jnp.stack([lax.axis_index("row"), lax.axis_index("tok_0")]).astype(jnp.int32)
+    partial = product(place, mine, other, rows, groups, units)
     received = exchange(partial.astype(jnp.float16), TOK)
     received = received.reshape(across, lower, padded, quarter)
     scale = jnp.exp2(received[:, :, units : units + 1, :1].astype(jnp.float32))

time: 133 us -> 124 us (0.932)
  the two profiles are of different devices: /device:TPU:24 before, /device:TPU:1 now
where the time goes in v2:
time: 124 us; the launch traced here: 122 us
  starting transfers between devices  58.4 us (47%)
  waiting for transfers between devices  29.1 us (23%)
  blocking collectives  22.8 us (18%)
  local copies, waits for them, and re-layouts  5.24 us (4%)
  Pallas kernels  4.08 us (3%)
  other arithmetic  2.17 us (2%)
    ppermute x7, starting transfers between devices, passed_on(): return lax.ppermute(array, ('row', 'col_1'), steps)  26.8 us
    all_to_all x1, blocking collectives, exchange(): return lax.all_to_all(blocks, axis, 0, 0, tiled=True)  22.8 us
    ppermute x4, waiting for transfers between devices, shifted(): lax.ppermute(array, axis, [(k, (k + by) % count) for k in range(count)])  18.7 us
    all_to_all x1, starting transfers between devices, exchange(): return lax.all_to_all(blocks, axis, 0, 0, tiled=True)  17.6 us
    ppermute x4, starting transfers between devices, shifted(): lax.ppermute(array, axis, [(k, (k + by) % count) for k in range(count)])  14 us
    ppermute x7, waiting for transfers between devices, passed_on(): return lax.ppermute(array, ('row', 'col_1'), steps)  10.4 us
    pallas_call x1, Pallas kernels, product(): pl.pallas_call(lambda *refs: product_kernel(*refs, units=units), out_shap...  4.08 us
  transfers between devices with their start and end apart: 12, of which 6 were waited for; matrix products, arithmetic and copies ran while one was open for 2% of the time, Pallas kernels for 0%

profile of v2, /device:TPU:1, one launch (start us, length us, event | category | flops | bytes accessed | tf_op | source)
XLA Modules:
  0.0 122.1 jit_solution(11962227180075188246)
XLA Ops:
  0.0 0.8 slice_bitcast_fusion.7
  0.8 0.7 broadcast_in_dim.37
  1.5 17.6 %all-to-all-start = ((bf16[16,16,512]{2,1,0:T(8,128)(2,1)}), bf16[16,16,512]{2,1,0:T(8,128)(2,1)S(1)}, u32[]{:S(2)}, u32[]{:S(2)}) async-start(bf16[16,16,512]{2,1,0:T(8,128)(2,1)} %bitcast.11), calls=%async_computation | async-start | bytes 524288 | tf_op jit(solution)/shard_map/all_to_all | solution.py:14
  19.1 1.1 pad.4
  20.2 3.3 %collective-permute-start = (bf16[960,256]{1,0:T(8,128)(2,1)S(1)}, bf16[960,256]{1,0:T(8,128)(2,1)S(1)}, u32[]{:S(2)}, u32[]{:S(2)}) collective-permute-start(bf16[960,256]{1,0:T(8,128)(2,1)S(1)} %bitcast.61), channel_id=1, source_target_pairs={{0,192},{192,384},{384,576},{576,0},{1,193},{193,385},{385,577},{5... | collective-permute-start | bytes 1474568 | tf_op jit(solution)/shard_map/ppermute | solution.py:19
  23.5 4.3 %collective-permute-start.1 = (bf16[960,256]{1,0:T(8,128)(2,1)S(1)}, bf16[960,256]{1,0:T(8,128)(2,1)S(1)}, u32[]{:S(2)}, u32[]{:S(2)}) collective-permute-start(bf16[960,256]{1,0:T(8,128)(2,1)S(1)} %bitcast.62), channel_id=1, source_target_pairs={{0,384},{192,576},{384,0},{576,192},{1,385},{193,577},{385,1},{577... | collective-permute-start | bytes 1474568 | tf_op jit(solution)/shard_map/ppermute | solution.py:19
  27.8 3.1 %collective-permute-start.2 = (bf16[960,256]{1,0:T(8,128)(2,1)S(1)}, bf16[960,256]{1,0:T(8,128)(2,1)S(1)}, u32[]{:S(2)}, u32[]{:S(2)}) collective-permute-start(bf16[960,256]{1,0:T(8,128)(2,1)S(1)} %bitcast.63), channel_id=1, source_target_pairs={{0,576},{192,0},{384,192},{576,384},{1,577},{193,1},{385,193},{577... | collective-permute-start | bytes 1474568 | tf_op jit(solution)/shard_map/ppermute | solution.py:19
  30.9 6.9 %collective-permute-done = bf16[960,256]{1,0:T(8,128)(2,1)S(1)} collective-permute-done((bf16[960,256]{1,0:T(8,128)(2,1)S(1)}, bf16[960,256]{1,0:T(8,128)(2,1)S(1)}, u32[]{:S(2)}, u32[]{:S(2)}) %collective-permute-start) | collective-permute-done | bytes 491552 | tf_op jit(solution)/shard_map/ppermute | solution.py:19
  37.8 11.4 %collective-permute-done.1 = bf16[960,256]{1,0:T(8,128)(2,1)S(1)} collective-permute-done((bf16[960,256]{1,0:T(8,128)(2,1)S(1)}, bf16[960,256]{1,0:T(8,128)(2,1)S(1)}, u32[]{:S(2)}, u32[]{:S(2)}) %collective-permute-start.1) | collective-permute-done | bytes 491552 | tf_op jit(solution)/shard_map/ppermute | solution.py:19
  49.1 0.5 collective-permute-done.2
  49.6 0.3 copy-done
  49.9 0.5 copy-done.1
  50.4 1.4 %pad_maximum_fusion.refs_1_ = bf16[4,960,256]{2,1,0:T(8,128)(2,1)S(1)} fusion(bf16[1,960,256]{2,1,0:T(8,128)(2,1)} %bitcast.67, bf16[1,960,256]{2,1,0:T(8,128)(2,1)} %bitcast.66, bf16[1,960,256]{2,1,0:T(8,128)(2,1)S(1)} %bitcast.65, bf16[1,960,256]{2,1,0:T(8,128)(2,1)S(1)} %bitcast.64), kind=kLoop, calls=%fused_computation | loop fusion | flops 2949120 | bytes 3932160 | tf_op jit(solution)/shard_map/stack | solution.py:103
  51.9 3.3 %collective-permute-start.3 = (bf16[4,960,256]{2,1,0:T(8,128)(2,1)S(1)}, bf16[4,960,256]{2,1,0:T(8,128)(2,1)}, u32[]{:S(2)}, u32[]{:S(2)}) collective-permute-start(bf16[4,960,256]{2,1,0:T(8,128)(2,1)S(1)} %pad_maximum_fusion.refs_1_), channel_id=1, source_target_pairs={{0,32},{32,0},{1,33},{33,1},{2,34},{34,2},{3,35},{35,3},{4,36},{36... | collective-permute-start | bytes 5898248 | tf_op jit(solution)/shard_map/ppermute | solution.py:19
  55.2 5.1 %collective-permute-start.4 = (bf16[16,16,512]{2,1,0:T(8,128)(2,1)S(1)}, bf16[16,16,512]{2,1,0:T(8,128)(2,1)S(1)}, u32[]{:S(2)}, u32[]{:S(2)}) collective-permute-start(bf16[16,16,512]{2,1,0:T(8,128)(2,1)S(1)} %all-to-all-done), channel_id=1, source_target_pairs={{0,1},{1,2},{2,3},{3,4},{4,5},{5,6},{6,7},{7,0},{32,39},{33,32},{3... | collective-permute-start | bytes 786440 | tf_op jit(solution)/shard_map/ppermute | solution.py:26
  60.3 3.8 %collective-permute-start.6 = (bf16[16,16,512]{2,1,0:T(8,128)(2,1)S(1)}, bf16[16,16,512]{2,1,0:T(8,128)(2,1)S(1)}, u32[]{:S(2)}, u32[]{:S(2)}) collective-permute-start(bf16[16,16,512]{2,1,0:T(8,128)(2,1)S(1)} %all-to-all-done), channel_id=1, source_target_pairs={{0,2},{1,3},{2,4},{3,5},{4,6},{5,7},{6,0},{7,1},{32,38},{33,39},{3... | collective-permute-start | bytes 786440 | tf_op jit(solution)/shard_map/ppermute | solution.py:26
  64.1 2.4 %collective-permute-start.7 = (bf16[16,16,512]{2,1,0:T(8,128)(2,1)S(1)}, bf16[16,16,512]{2,1,0:T(8,128)(2,1)S(1)}, u32[]{:S(2)}, u32[]{:S(2)}) collective-permute-start(bf16[16,16,512]{2,1,0:T(8,128)(2,1)S(1)} %all-to-all-done), channel_id=1, source_target_pairs={{0,6},{1,7},{2,0},{3,1},{4,2},{5,3},{6,4},{7,5},{32,34},{33,35},{3... | collective-permute-start | bytes 786440 | tf_op jit(solution)/shard_map/ppermute | solution.py:26
  66.5 0.1 pad_add_fusion.refs_0_
  66.6 1.9 %collective-permute-start.5 = (bf16[16,16,512]{2,1,0:T(8,128)(2,1)S(1)}, bf16[16,16,512]{2,1,0:T(8,128)(2,1)S(1)}, u32[]{:S(2)}, u32[]{:S(2)}) collective-permute-start(bf16[16,16,512]{2,1,0:T(8,128)(2,1)S(1)} %all-to-all-done), channel_id=1, source_target_pairs={{0,7},{1,0},{2,1},{3,2},{4,3},{5,4},{6,5},{7,6},{32,33},{33,34},{3... | collective-permute-start | bytes 786440 | tf_op jit(solution)/shard_map/ppermute | solution.py:26
  68.6 0.3 broadcast_in_dim.36
  68.9 2.3 %collective-permute-done.6 = bf16[16,16,512]{2,1,0:T(8,128)(2,1)S(1)} collective-permute-done((bf16[16,16,512]{2,1,0:T(8,128)(2,1)S(1)}, bf16[16,16,512]{2,1,0:T(8,128)(2,1)S(1)}, u32[]{:S(2)}, u32[]{:S(2)}) %collective-permute-start.6) | collective-permute-done | bytes 262176 | tf_op jit(solution)/shard_map/ppermute | solution.py:26
  71.1 8.5 %collective-permute-start.8 = (bf16[16,16,512]{2,1,0:T(8,128)(2,1)S(1)}, bf16[16,16,512]{2,1,0:T(8,128)(2,1)S(1)}, u32[]{:S(2)}, u32[]{:S(2)}) collective-permute-start(bf16[16,16,512]{2,1,0:T(8,128)(2,1)S(1)} %collective-permute-done.6), channel_id=1, source_target_pairs={{0,1},{1,2},{2,3},{3,4},{4,5},{5,6},{6,7},{7,0},{32,39},{33,32},{3... | collective-permute-start | bytes 786440 | tf_op jit(solution)/shard_map/ppermute | solution.py:26
  79.7 1.9 %collective-permute-start.9 = (bf16[16,16,512]{2,1,0:T(8,128)(2,1)S(1)}, bf16[16,16,512]{2,1,0:T(8,128)(2,1)S(1)}, u32[]{:S(2)}, u32[]{:S(2)}) collective-permute-start(bf16[16,16,512]{2,1,0:T(8,128)(2,1)S(1)} %collective-permute-done.6), channel_id=1, source_target_pairs={{0,2},{1,3},{2,4},{3,5},{4,6},{5,7},{6,0},{7,1},{32,38},{33,39},{3... | collective-permute-start | bytes 786440 | tf_op jit(solution)/shard_map/ppermute | solution.py:26
  81.6 3.1 %collective-permute-start.10 = (bf16[16,16,512]{2,1,0:T(8,128)(2,1)S(1)}, bf16[16,16,512]{2,1,0:T(8,128)(2,1)S(1)}, u32[]{:S(2)}, u32[]{:S(2)}) collective-permute-start(bf16[16,16,512]{2,1,0:T(8,128)(2,1)S(1)} %collective-permute-done.7), channel_id=1, source_target_pairs={{0,7},{1,0},{2,1},{3,2},{4,3},{5,4},{6,5},{7,6},{32,33},{33,34},{3... | collective-permute-start | bytes 786440 | tf_op jit(solution)/shard_map/ppermute | solution.py:26
  84.9 5.1 %collective-permute-done.9 = bf16[16,16,512]{2,1,0:T(8,128)(2,1)S(1)} collective-permute-done((bf16[16,16,512]{2,1,0:T(8,128)(2,1)S(1)}, bf16[16,16,512]{2,1,0:T(8,128)(2,1)S(1)}, u32[]{:S(2)}, u32[]{:S(2)}) %collective-permute-start.9) | collective-permute-done | bytes 262176 | tf_op jit(solution)/shard_map/ppermute | solution.py:26
  90.0 3.1 %collective-permute-done.10 = bf16[16,16,512]{2,1,0:T(8,128)(2,1)S(1)} collective-permute-done((bf16[16,16,512]{2,1,0:T(8,128)(2,1)S(1)}, bf16[16,16,512]{2,1,0:T(8,128)(2,1)S(1)}, u32[]{:S(2)}, u32[]{:S(2)}) %collective-permute-start.10) | collective-permute-done | bytes 262176 | tf_op jit(solution)/shard_map/ppermute | solution.py:26
  93.1 4.1 %product.1 = f32[12,80,512]{2,1,0:T(8,128)S(1)} custom-call(s32[2]{0:T(128)S(1)} %pad_add_fusion.refs_0_, bf16[4,960,256]{2,1,0:T(8,128)(2,1)S(1)} %pad_maximum_fusion.refs_1_, bf16[4,960,256]{2,1,0:T(8,128)(2,1)} %collective-permute-done.3.refs_2_, bf16[2048,512]{1,0:T(8,128)(2,1)S(1)} %bitcast.58), custom_call_target="tpu_custom_call" | custom-call | tf_op jit(solution)/shard_map/product/pallas_call | solution.py:75
  97.2 0.2 convert_element_type.11
  97.4 22.8 %all_to_all.10 = f16[12,80,512]{2,1,0:T(8,128)(2,1)S(1)} all-to-all(f16[12,80,512]{2,1,0:T(8,128)(2,1)S(1)} %convert_element_type.11), channel_id=1, replica_groups=mesh['tok_0'=4,'tok_1'=3,'row'=2,'col_0'=4,'col_1'=8] {'tok_0','tok_1'}, dimensions={0} | all-to-all | bytes 1966080 | tf_op jit(solution)/shard_map/all_to_all | solution.py:14
  120.2 0.1 copy.11
  120.3 0.4 multiply_reduce_fusion
  120.8 1.3 %broadcast_in_dim.46 = f32[1,77,2048]{2,0,1:T(1,128)} reshape(f32[77,2048]{1,0:T(8,128)S(1)} %pad_maximum_fusion.1) | data formatting | bytes 1261568 | tf_op jit(solution)/shard_map/broadcast_in_dim | solution.py:111
  (21 shorter events, 0.3 us)
Async XLA Ops:
  1.5 53.7 %all-to-all-start = ((bf16[16,16,512]{2,1,0:T(8,128)(2,1)}), bf16[16,16,512]{2,1,0:T(8,128)(2,1)S(1)}, u32[]{:S(2)}, u32[]{:S(2)}) async-start(bf16[16,16,512]{2,1,0:T(8,128)(2,1)} %bitcast.11), calls=%async_computation | async-start | bytes 524288 | tf_op jit(solution)/shard_map/all_to_all | solution.py:14
  20.2 17.6 %collective-permute-start = (bf16[960,256]{1,0:T(8,128)(2,1)S(1)}, bf16[960,256]{1,0:T(8,128)(2,1)S(1)}, u32[]{:S(2)}, u32[]{:S(2)}) collective-permute-start(bf16[960,256]{1,0:T(8,128)(2,1)S(1)} %bitcast.61), channel_id=1, source_target_pairs={{0,192},{192,384},{384,576},{576,0},{1,193},{193,385},{385,577},{5... | collective-permute-start | bytes 1474568 | tf_op jit(solution)/shard_map/ppermute | solution.py:19
  23.5 25.6 %collective-permute-start.1 = (bf16[960,256]{1,0:T(8,128)(2,1)S(1)}, bf16[960,256]{1,0:T(8,128)(2,1)S(1)}, u32[]{:S(2)}, u32[]{:S(2)}) collective-permute-start(bf16[960,256]{1,0:T(8,128)(2,1)S(1)} %bitcast.62), channel_id=1, source_target_pairs={{0,384},{192,576},{384,0},{576,192},{1,385},{193,577},{385,1},{577... | collective-permute-start | bytes 1474568 | tf_op jit(solution)/shard_map/ppermute | solution.py:19
  27.8 21.8 %collective-permute-start.2 = (bf16[960,256]{1,0:T(8,128)(2,1)S(1)}, bf16[960,256]{1,0:T(8,128)(2,1)S(1)}, u32[]{:S(2)}, u32[]{:S(2)}) collective-permute-start(bf16[960,256]{1,0:T(8,128)(2,1)S(1)} %bitcast.63), channel_id=1, source_target_pairs={{0,576},{192,0},{384,192},{576,384},{1,577},{193,1},{385,193},{577... | collective-permute-start | bytes 1474568 | tf_op jit(solution)/shard_map/ppermute | solution.py:19
  49.1 0.8 copy-start
  49.6 0.8 copy-start.1
  51.9 41.2 %collective-permute-start.3 = (bf16[4,960,256]{2,1,0:T(8,128)(2,1)S(1)}, bf16[4,960,256]{2,1,0:T(8,128)(2,1)}, u32[]{:S(2)}, u32[]{:S(2)}) collective-permute-start(bf16[4,960,256]{2,1,0:T(8,128)(2,1)S(1)} %pad_maximum_fusion.refs_1_), channel_id=1, source_target_pairs={{0,32},{32,0},{1,33},{33,1},{2,34},{34,2},{3,35},{35,3},{4,36},{36... | collective-permute-start | bytes 5898248 | tf_op jit(solution)/shard_map/ppermute | solution.py:19
  55.2 24.5 %collective-permute-start.4 = (bf16[16,16,512]{2,1,0:T(8,128)(2,1)S(1)}, bf16[16,16,512]{2,1,0:T(8,128)(2,1)S(1)}, u32[]{:S(2)}, u32[]{:S(2)}) collective-permute-start(bf16[16,16,512]{2,1,0:T(8,128)(2,1)S(1)} %all-to-all-done), channel_id=1, source_target_pairs={{0,1},{1,2},{2,3},{3,4},{4,5},{5,6},{6,7},{7,0},{32,39},{33,32},{3... | collective-permute-start | bytes 786440 | tf_op jit(solution)/shard_map/ppermute | solution.py:26
  60.3 10.8 %collective-permute-start.6 = (bf16[16,16,512]{2,1,0:T(8,128)(2,1)S(1)}, bf16[16,16,512]{2,1,0:T(8,128)(2,1)S(1)}, u32[]{:S(2)}, u32[]{:S(2)}) collective-permute-start(bf16[16,16,512]{2,1,0:T(8,128)(2,1)S(1)} %all-to-all-done), channel_id=1, source_target_pairs={{0,2},{1,3},{2,4},{3,5},{4,6},{5,7},{6,0},{7,1},{32,38},{33,39},{3... | collective-permute-start | bytes 786440 | tf_op jit(solution)/shard_map/ppermute | solution.py:26
  64.1 17.5 %collective-permute-start.7 = (bf16[16,16,512]{2,1,0:T(8,128)(2,1)S(1)}, bf16[16,16,512]{2,1,0:T(8,128)(2,1)S(1)}, u32[]{:S(2)}, u32[]{:S(2)}) collective-permute-start(bf16[16,16,512]{2,1,0:T(8,128)(2,1)S(1)} %all-to-all-done), channel_id=1, source_target_pairs={{0,6},{1,7},{2,0},{3,1},{4,2},{5,3},{6,4},{7,5},{32,34},{33,35},{3... | collective-permute-start | bytes 786440 | tf_op jit(solution)/shard_map/ppermute | solution.py:26
  66.6 18.1 %collective-permute-start.5 = (bf16[16,16,512]{2,1,0:T(8,128)(2,1)S(1)}, bf16[16,16,512]{2,1,0:T(8,128)(2,1)S(1)}, u32[]{:S(2)}, u32[]{:S(2)}) collective-permute-start(bf16[16,16,512]{2,1,0:T(8,128)(2,1)S(1)} %all-to-all-done), channel_id=1, source_target_pairs={{0,7},{1,0},{2,1},{3,2},{4,3},{5,4},{6,5},{7,6},{32,33},{33,34},{3... | collective-permute-start | bytes 786440 | tf_op jit(solution)/shard_map/ppermute | solution.py:26
  71.1 13.7 %collective-permute-start.8 = (bf16[16,16,512]{2,1,0:T(8,128)(2,1)S(1)}, bf16[16,16,512]{2,1,0:T(8,128)(2,1)S(1)}, u32[]{:S(2)}, u32[]{:S(2)}) collective-permute-start(bf16[16,16,512]{2,1,0:T(8,128)(2,1)S(1)} %collective-permute-done.6), channel_id=1, source_target_pairs={{0,1},{1,2},{2,3},{3,4},{4,5},{5,6},{6,7},{7,0},{32,39},{33,32},{3... | collective-permute-start | bytes 786440 | tf_op jit(solution)/shard_map/ppermute | solution.py:26
  79.7 10.3 %collective-permute-start.9 = (bf16[16,16,512]{2,1,0:T(8,128)(2,1)S(1)}, bf16[16,16,512]{2,1,0:T(8,128)(2,1)S(1)}, u32[]{:S(2)}, u32[]{:S(2)}) collective-permute-start(bf16[16,16,512]{2,1,0:T(8,128)(2,1)S(1)} %collective-permute-done.6), channel_id=1, source_target_pairs={{0,2},{1,3},{2,4},{3,5},{4,6},{5,7},{6,0},{7,1},{32,38},{33,39},{3... | collective-permute-start | bytes 786440 | tf_op jit(solution)/shard_map/ppermute | solution.py:26
  81.6 11.4 %collective-permute-start.10 = (bf16[16,16,512]{2,1,0:T(8,128)(2,1)S(1)}, bf16[16,16,512]{2,1,0:T(8,128)(2,1)S(1)}, u32[]{:S(2)}, u32[]{:S(2)}) collective-permute-start(bf16[16,16,512]{2,1,0:T(8,128)(2,1)S(1)} %collective-permute-done.7), channel_id=1, source_target_pairs={{0,7},{1,0},{2,1},{3,2},{4,3},{5,4},{6,5},{7,6},{32,33},{33,34},{3... | collective-permute-start | bytes 786440 | tf_op jit(solution)/shard_map/ppermute | solution.py:26

commit v3 on v2

--- a/solution.py
+++ b/solution.py
@@ -46,18 +46,21 @@
 
 
 def product_kernel(place_ref, mine_ref, other_ref, rows_ref, out_ref, total_ref, *, units):
-    blocks, _, depth = mine_ref.shape
+    blocks, height, depth = mine_ref.shape
     side, across = place_ref[0], place_ref[1]
+    starts = []
     for k in range(blocks):
         first = 2 * lax.rem(across + blocks - k, blocks)
-        own = rows_ref[pl.ds(pl.multiple_of((first + side) * depth, depth), depth), :]
-        far = rows_ref[pl.ds(pl.multiple_of((first + 1 - side) * depth, depth), depth), :]
-        add = jnp.dot(mine_ref[k], own, preferred_element_type=jnp.float32)
-        add += jnp.dot(other_ref[k], far, preferred_element_type=jnp.float32)
-        if k == 0:
-            total_ref[...] = add
-        else:
-            total_ref[...] += add
+        starts.append([pl.multiple_of((first + half) * depth, depth) for half in (side, 1 - side)])
+    tile = height // 4
+    for m in range(4):
+        part = slice(m * tile, (m + 1) * tile)
+        add = None
+        for k, (own, far) in enumerate(starts):
+            for blocks_ref, start in ((mine_ref, own), (other_ref, far)):
+                term = jnp.dot(blocks_ref[k, part], rows_ref[pl.ds(start, depth), :], preferred_element_type=jnp.float32)
+                add = term if add is None else add + term
+        total_ref[part, :] = add
     limit = jnp.maximum(jnp.max(jnp.abs(total_ref[...])), 1e-30)
     exponent = jnp.ceil(jnp.log2(jnp.full((1, 128), limit, jnp.float32))) - 15.0
     exponent = jnp.max(exponent)

time: 124 us -> 124 us (level)
  no operation moved by 1% of the time
where the time goes in v3:
time: 124 us; the launch traced here: 122 us
  starting transfers between devices  58.4 us (47%)
  waiting for transfers between devices  29.1 us (23%)
  blocking collectives  22.8 us (18%)
  local copies, waits for them, and re-layouts  5.24 us (4%)
  Pallas kernels  4.08 us (3%)
  other arithmetic  2.17 us (2%)
    ppermute x7, starting transfers between devices, passed_on(): return lax.ppermute(array, ('row', 'col_1'), steps)  26.8 us
    all_to_all x1, blocking collectives, exchange(): return lax.all_to_all(blocks, axis, 0, 0, tiled=True)  22.8 us
    ppermute x4, waiting for transfers between devices, shifted(): lax.ppermute(array, axis, [(k, (k + by) % count) for k in range(count)])  18.7 us
    all_to_all x1, starting transfers between devices, exchange(): return lax.all_to_all(blocks, axis, 0, 0, tiled=True)  17.6 us
    ppermute x4, starting transfers between devices, shifted(): lax.ppermute(array, axis, [(k, (k + by) % count) for k in range(count)])  14 us
    ppermute x7, waiting for transfers between devices, passed_on(): return lax.ppermute(array, ('row', 'col_1'), steps)  10.4 us
    pallas_call x1, Pallas kernels, product(): pl.pallas_call(lambda *refs: product_kernel(*refs, units=units), out_shap...  4.08 us
  transfers between devices with their start and end apart: 12, of which 6 were waited for; matrix products, arithmetic and copies ran while one was open for 2% of the time, Pallas kernels for 0%

profile of v3, /device:TPU:1, one launch (start us, length us, event | category | flops | bytes accessed | tf_op | source)
XLA Modules:
  0.0 122.1 jit_solution(3615311510105836123)
XLA Ops:
  0.0 0.8 slice_bitcast_fusion.7
  0.8 0.7 broadcast_in_dim.37
  1.5 17.6 %all-to-all-start = ((bf16[16,16,512]{2,1,0:T(8,128)(2,1)}), bf16[16,16,512]{2,1,0:T(8,128)(2,1)S(1)}, u32[]{:S(2)}, u32[]{:S(2)}) async-start(bf16[16,16,512]{2,1,0:T(8,128)(2,1)} %bitcast.11), calls=%async_computation | async-start | bytes 524288 | tf_op jit(solution)/shard_map/all_to_all | solution.py:14
  19.1 1.1 pad.4
  20.2 3.3 %collective-permute-start = (bf16[960,256]{1,0:T(8,128)(2,1)S(1)}, bf16[960,256]{1,0:T(8,128)(2,1)S(1)}, u32[]{:S(2)}, u32[]{:S(2)}) collective-permute-start(bf16[960,256]{1,0:T(8,128)(2,1)S(1)} %bitcast.61), channel_id=1, source_target_pairs={{0,192},{192,384},{384,576},{576,0},{1,193},{193,385},{385,577},{5... | collective-permute-start | bytes 1474568 | tf_op jit(solution)/shard_map/ppermute | solution.py:19
  23.5 4.3 %collective-permute-start.1 = (bf16[960,256]{1,0:T(8,128)(2,1)S(1)}, bf16[960,256]{1,0:T(8,128)(2,1)S(1)}, u32[]{:S(2)}, u32[]{:S(2)}) collective-permute-start(bf16[960,256]{1,0:T(8,128)(2,1)S(1)} %bitcast.62), channel_id=1, source_target_pairs={{0,384},{192,576},{384,0},{576,192},{1,385},{193,577},{385,1},{577... | collective-permute-start | bytes 1474568 | tf_op jit(solution)/shard_map/ppermute | solution.py:19
  27.8 3.1 %collective-permute-start.2 = (bf16[960,256]{1,0:T(8,128)(2,1)S(1)}, bf16[960,256]{1,0:T(8,128)(2,1)S(1)}, u32[]{:S(2)}, u32[]{:S(2)}) collective-permute-start(bf16[960,256]{1,0:T(8,128)(2,1)S(1)} %bitcast.63), channel_id=1, source_target_pairs={{0,576},{192,0},{384,192},{576,384},{1,577},{193,1},{385,193},{577... | collective-permute-start | bytes 1474568 | tf_op jit(solution)/shard_map/ppermute | solution.py:19
  30.9 6.9 %collective-permute-done = bf16[960,256]{1,0:T(8,128)(2,1)S(1)} collective-permute-done((bf16[960,256]{1,0:T(8,128)(2,1)S(1)}, bf16[960,256]{1,0:T(8,128)(2,1)S(1)}, u32[]{:S(2)}, u32[]{:S(2)}) %collective-permute-start) | collective-permute-done | bytes 491552 | tf_op jit(solution)/shard_map/ppermute | solution.py:19
  37.8 11.4 %collective-permute-done.1 = bf16[960,256]{1,0:T(8,128)(2,1)S(1)} collective-permute-done((bf16[960,256]{1,0:T(8,128)(2,1)S(1)}, bf16[960,256]{1,0:T(8,128)(2,1)S(1)}, u32[]{:S(2)}, u32[]{:S(2)}) %collective-permute-start.1) | collective-permute-done | bytes 491552 | tf_op jit(solution)/shard_map/ppermute | solution.py:19
  49.1 0.5 collective-permute-done.2
  49.6 0.3 copy-done
  49.9 0.5 copy-done.1
  50.4 1.4 %pad_maximum_fusion.refs_1_ = bf16[4,960,256]{2,1,0:T(8,128)(2,1)S(1)} fusion(bf16[1,960,256]{2,1,0:T(8,128)(2,1)} %bitcast.67, bf16[1,960,256]{2,1,0:T(8,128)(2,1)} %bitcast.66, bf16[1,960,256]{2,1,0:T(8,128)(2,1)S(1)} %bitcast.65, bf16[1,960,256]{2,1,0:T(8,128)(2,1)S(1)} %bitcast.64), kind=kLoop, calls=%fused_computation | loop fusion | flops 2949120 | bytes 3932160 | tf_op jit(solution)/shard_map/stack | solution.py:106
  51.9 3.3 %collective-permute-start.3 = (bf16[4,960,256]{2,1,0:T(8,128)(2,1)S(1)}, bf16[4,960,256]{2,1,0:T(8,128)(2,1)}, u32[]{:S(2)}, u32[]{:S(2)}) collective-permute-start(bf16[4,960,256]{2,1,0:T(8,128)(2,1)S(1)} %pad_maximum_fusion.refs_1_), channel_id=1, source_target_pairs={{0,32},{32,0},{1,33},{33,1},{2,34},{34,2},{3,35},{35,3},{4,36},{36... | collective-permute-start | bytes 5898248 | tf_op jit(solution)/shard_map/ppermute | solution.py:19
  55.2 5.1 %collective-permute-start.4 = (bf16[16,16,512]{2,1,0:T(8,128)(2,1)S(1)}, bf16[16,16,512]{2,1,0:T(8,128)(2,1)S(1)}, u32[]{:S(2)}, u32[]{:S(2)}) collective-permute-start(bf16[16,16,512]{2,1,0:T(8,128)(2,1)S(1)} %all-to-all-done), channel_id=1, source_target_pairs={{0,1},{1,2},{2,3},{3,4},{4,5},{5,6},{6,7},{7,0},{32,39},{33,32},{3... | collective-permute-start | bytes 786440 | tf_op jit(solution)/shard_map/ppermute | solution.py:26
  60.3 3.8 %collective-permute-start.6 = (bf16[16,16,512]{2,1,0:T(8,128)(2,1)S(1)}, bf16[16,16,512]{2,1,0:T(8,128)(2,1)S(1)}, u32[]{:S(2)}, u32[]{:S(2)}) collective-permute-start(bf16[16,16,512]{2,1,0:T(8,128)(2,1)S(1)} %all-to-all-done), channel_id=1, source_target_pairs={{0,2},{1,3},{2,4},{3,5},{4,6},{5,7},{6,0},{7,1},{32,38},{33,39},{3... | collective-permute-start | bytes 786440 | tf_op jit(solution)/shard_map/ppermute | solution.py:26
  64.1 2.4 %collective-permute-start.7 = (bf16[16,16,512]{2,1,0:T(8,128)(2,1)S(1)}, bf16[16,16,512]{2,1,0:T(8,128)(2,1)S(1)}, u32[]{:S(2)}, u32[]{:S(2)}) collective-permute-start(bf16[16,16,512]{2,1,0:T(8,128)(2,1)S(1)} %all-to-all-done), channel_id=1, source_target_pairs={{0,6},{1,7},{2,0},{3,1},{4,2},{5,3},{6,4},{7,5},{32,34},{33,35},{3... | collective-permute-start | bytes 786440 | tf_op jit(solution)/shard_map/ppermute | solution.py:26
  66.5 0.1 pad_add_fusion.refs_0_
  66.6 1.9 %collective-permute-start.5 = (bf16[16,16,512]{2,1,0:T(8,128)(2,1)S(1)}, bf16[16,16,512]{2,1,0:T(8,128)(2,1)S(1)}, u32[]{:S(2)}, u32[]{:S(2)}) collective-permute-start(bf16[16,16,512]{2,1,0:T(8,128)(2,1)S(1)} %all-to-all-done), channel_id=1, source_target_pairs={{0,7},{1,0},{2,1},{3,2},{4,3},{5,4},{6,5},{7,6},{32,33},{33,34},{3... | collective-permute-start | bytes 786440 | tf_op jit(solution)/shard_map/ppermute | solution.py:26
  68.6 0.3 broadcast_in_dim.36
  68.9 2.3 %collective-permute-done.6 = bf16[16,16,512]{2,1,0:T(8,128)(2,1)S(1)} collective-permute-done((bf16[16,16,512]{2,1,0:T(8,128)(2,1)S(1)}, bf16[16,16,512]{2,1,0:T(8,128)(2,1)S(1)}, u32[]{:S(2)}, u32[]{:S(2)}) %collective-permute-start.6) | collective-permute-done | bytes 262176 | tf_op jit(solution)/shard_map/ppermute | solution.py:26
  71.1 8.5 %collective-permute-start.8 = (bf16[16,16,512]{2,1,0:T(8,128)(2,1)S(1)}, bf16[16,16,512]{2,1,0:T(8,128)(2,1)S(1)}, u32[]{:S(2)}, u32[]{:S(2)}) collective-permute-start(bf16[16,16,512]{2,1,0:T(8,128)(2,1)S(1)} %collective-permute-done.6), channel_id=1, source_target_pairs={{0,1},{1,2},{2,3},{3,4},{4,5},{5,6},{6,7},{7,0},{32,39},{33,32},{3... | collective-permute-start | bytes 786440 | tf_op jit(solution)/shard_map/ppermute | solution.py:26
  79.7 1.9 %collective-permute-start.9 = (bf16[16,16,512]{2,1,0:T(8,128)(2,1)S(1)}, bf16[16,16,512]{2,1,0:T(8,128)(2,1)S(1)}, u32[]{:S(2)}, u32[]{:S(2)}) collective-permute-start(bf16[16,16,512]{2,1,0:T(8,128)(2,1)S(1)} %collective-permute-done.6), channel_id=1, source_target_pairs={{0,2},{1,3},{2,4},{3,5},{4,6},{5,7},{6,0},{7,1},{32,38},{33,39},{3... | collective-permute-start | bytes 786440 | tf_op jit(solution)/shard_map/ppermute | solution.py:26
  81.6 3.1 %collective-permute-start.10 = (bf16[16,16,512]{2,1,0:T(8,128)(2,1)S(1)}, bf16[16,16,512]{2,1,0:T(8,128)(2,1)S(1)}, u32[]{:S(2)}, u32[]{:S(2)}) collective-permute-start(bf16[16,16,512]{2,1,0:T(8,128)(2,1)S(1)} %collective-permute-done.7), channel_id=1, source_target_pairs={{0,7},{1,0},{2,1},{3,2},{4,3},{5,4},{6,5},{7,6},{32,33},{33,34},{3... | collective-permute-start | bytes 786440 | tf_op jit(solution)/shard_map/ppermute | solution.py:26
  84.9 5.1 %collective-permute-done.9 = bf16[16,16,512]{2,1,0:T(8,128)(2,1)S(1)} collective-permute-done((bf16[16,16,512]{2,1,0:T(8,128)(2,1)S(1)}, bf16[16,16,512]{2,1,0:T(8,128)(2,1)S(1)}, u32[]{:S(2)}, u32[]{:S(2)}) %collective-permute-start.9) | collective-permute-done | bytes 262176 | tf_op jit(solution)/shard_map/ppermute | solution.py:26
  90.0 3.1 %collective-permute-done.10 = bf16[16,16,512]{2,1,0:T(8,128)(2,1)S(1)} collective-permute-done((bf16[16,16,512]{2,1,0:T(8,128)(2,1)S(1)}, bf16[16,16,512]{2,1,0:T(8,128)(2,1)S(1)}, u32[]{:S(2)}, u32[]{:S(2)}) %collective-permute-start.10) | collective-permute-done | bytes 262176 | tf_op jit(solution)/shard_map/ppermute | solution.py:26
  93.1 4.1 %product.1 = f32[12,80,512]{2,1,0:T(8,128)S(1)} custom-call(s32[2]{0:T(128)S(1)} %pad_add_fusion.refs_0_, bf16[4,960,256]{2,1,0:T(8,128)(2,1)S(1)} %pad_maximum_fusion.refs_1_, bf16[4,960,256]{2,1,0:T(8,128)(2,1)} %collective-permute-done.3.refs_2_, bf16[2048,512]{1,0:T(8,128)(2,1)S(1)} %bitcast.58), custom_call_target="tpu_custom_call" | custom-call | tf_op jit(solution)/shard_map/product/pallas_call | solution.py:78
  97.2 0.2 convert_element_type.11
  97.4 22.8 %all_to_all.10 = f16[12,80,512]{2,1,0:T(8,128)(2,1)S(1)} all-to-all(f16[12,80,512]{2,1,0:T(8,128)(2,1)S(1)} %convert_element_type.11), channel_id=1, replica_groups=mesh['tok_0'=4,'tok_1'=3,'row'=2,'col_0'=4,'col_1'=8] {'tok_0','tok_1'}, dimensions={0} | all-to-all | bytes 1966080 | tf_op jit(solution)/shard_map/all_to_all | solution.py:14
  120.2 0.1 copy.11
  120.3 0.4 multiply_reduce_fusion
  120.8 1.3 %broadcast_in_dim.46 = f32[1,77,2048]{2,0,1:T(1,128)} reshape(f32[77,2048]{1,0:T(8,128)S(1)} %pad_maximum_fusion.1) | data formatting | bytes 1261568 | tf_op jit(solution)/shard_map/broadcast_in_dim | solution.py:114
  (21 shorter events, 0.3 us)
Async XLA Ops:
  1.5 53.7 %all-to-all-start = ((bf16[16,16,512]{2,1,0:T(8,128)(2,1)}), bf16[16,16,512]{2,1,0:T(8,128)(2,1)S(1)}, u32[]{:S(2)}, u32[]{:S(2)}) async-start(bf16[16,16,512]{2,1,0:T(8,128)(2,1)} %bitcast.11), calls=%async_computation | async-start | bytes 524288 | tf_op jit(solution)/shard_map/all_to_all | solution.py:14
  20.2 17.6 %collective-permute-start = (bf16[960,256]{1,0:T(8,128)(2,1)S(1)}, bf16[960,256]{1,0:T(8,128)(2,1)S(1)}, u32[]{:S(2)}, u32[]{:S(2)}) collective-permute-start(bf16[960,256]{1,0:T(8,128)(2,1)S(1)} %bitcast.61), channel_id=1, source_target_pairs={{0,192},{192,384},{384,576},{576,0},{1,193},{193,385},{385,577},{5... | collective-permute-start | bytes 1474568 | tf_op jit(solution)/shard_map/ppermute | solution.py:19
  23.5 25.6 %collective-permute-start.1 = (bf16[960,256]{1,0:T(8,128)(2,1)S(1)}, bf16[960,256]{1,0:T(8,128)(2,1)S(1)}, u32[]{:S(2)}, u32[]{:S(2)}) collective-permute-start(bf16[960,256]{1,0:T(8,128)(2,1)S(1)} %bitcast.62), channel_id=1, source_target_pairs={{0,384},{192,576},{384,0},{576,192},{1,385},{193,577},{385,1},{577... | collective-permute-start | bytes 1474568 | tf_op jit(solution)/shard_map/ppermute | solution.py:19
  27.8 21.8 %collective-permute-start.2 = (bf16[960,256]{1,0:T(8,128)(2,1)S(1)}, bf16[960,256]{1,0:T(8,128)(2,1)S(1)}, u32[]{:S(2)}, u32[]{:S(2)}) collective-permute-start(bf16[960,256]{1,0:T(8,128)(2,1)S(1)} %bitcast.63), channel_id=1, source_target_pairs={{0,576},{192,0},{384,192},{576,384},{1,577},{193,1},{385,193},{577... | collective-permute-start | bytes 1474568 | tf_op jit(solution)/shard_map/ppermute | solution.py:19
  49.1 0.8 copy-start
  49.6 0.8 copy-start.1
  51.9 41.2 %collective-permute-start.3 = (bf16[4,960,256]{2,1,0:T(8,128)(2,1)S(1)}, bf16[4,960,256]{2,1,0:T(8,128)(2,1)}, u32[]{:S(2)}, u32[]{:S(2)}) collective-permute-start(bf16[4,960,256]{2,1,0:T(8,128)(2,1)S(1)} %pad_maximum_fusion.refs_1_), channel_id=1, source_target_pairs={{0,32},{32,0},{1,33},{33,1},{2,34},{34,2},{3,35},{35,3},{4,36},{36... | collective-permute-start | bytes 5898248 | tf_op jit(solution)/shard_map/ppermute | solution.py:19
  55.2 24.5 %collective-permute-start.4 = (bf16[16,16,512]{2,1,0:T(8,128)(2,1)S(1)}, bf16[16,16,512]{2,1,0:T(8,128)(2,1)S(1)}, u32[]{:S(2)}, u32[]{:S(2)}) collective-permute-start(bf16[16,16,512]{2,1,0:T(8,128)(2,1)S(1)} %all-to-all-done), channel_id=1, source_target_pairs={{0,1},{1,2},{2,3},{3,4},{4,5},{5,6},{6,7},{7,0},{32,39},{33,32},{3... | collective-permute-start | bytes 786440 | tf_op jit(solution)/shard_map/ppermute | solution.py:26
  60.3 10.8 %collective-permute-start.6 = (bf16[16,16,512]{2,1,0:T(8,128)(2,1)S(1)}, bf16[16,16,512]{2,1,0:T(8,128)(2,1)S(1)}, u32[]{:S(2)}, u32[]{:S(2)}) collective-permute-start(bf16[16,16,512]{2,1,0:T(8,128)(2,1)S(1)} %all-to-all-done), channel_id=1, source_target_pairs={{0,2},{1,3},{2,4},{3,5},{4,6},{5,7},{6,0},{7,1},{32,38},{33,39},{3... | collective-permute-start | bytes 786440 | tf_op jit(solution)/shard_map/ppermute | solution.py:26
  64.1 17.5 %collective-permute-start.7 = (bf16[16,16,512]{2,1,0:T(8,128)(2,1)S(1)}, bf16[16,16,512]{2,1,0:T(8,128)(2,1)S(1)}, u32[]{:S(2)}, u32[]{:S(2)}) collective-permute-start(bf16[16,16,512]{2,1,0:T(8,128)(2,1)S(1)} %all-to-all-done), channel_id=1, source_target_pairs={{0,6},{1,7},{2,0},{3,1},{4,2},{5,3},{6,4},{7,5},{32,34},{33,35},{3... | collective-permute-start | bytes 786440 | tf_op jit(solution)/shard_map/ppermute | solution.py:26
  66.6 18.1 %collective-permute-start.5 = (bf16[16,16,512]{2,1,0:T(8,128)(2,1)S(1)}, bf16[16,16,512]{2,1,0:T(8,128)(2,1)S(1)}, u32[]{:S(2)}, u32[]{:S(2)}) collective-permute-start(bf16[16,16,512]{2,1,0:T(8,128)(2,1)S(1)} %all-to-all-done), channel_id=1, source_target_pairs={{0,7},{1,0},{2,1},{3,2},{4,3},{5,4},{6,5},{7,6},{32,33},{33,34},{3... | collective-permute-start | bytes 786440 | tf_op jit(solution)/shard_map/ppermute | solution.py:26
  71.1 13.7 %collective-permute-start.8 = (bf16[16,16,512]{2,1,0:T(8,128)(2,1)S(1)}, bf16[16,16,512]{2,1,0:T(8,128)(2,1)S(1)}, u32[]{:S(2)}, u32[]{:S(2)}) collective-permute-start(bf16[16,16,512]{2,1,0:T(8,128)(2,1)S(1)} %collective-permute-done.6), channel_id=1, source_target_pairs={{0,1},{1,2},{2,3},{3,4},{4,5},{5,6},{6,7},{7,0},{32,39},{33,32},{3... | collective-permute-start | bytes 786440 | tf_op jit(solution)/shard_map/ppermute | solution.py:26
  79.7 10.3 %collective-permute-start.9 = (bf16[16,16,512]{2,1,0:T(8,128)(2,1)S(1)}, bf16[16,16,512]{2,1,0:T(8,128)(2,1)S(1)}, u32[]{:S(2)}, u32[]{:S(2)}) collective-permute-start(bf16[16,16,512]{2,1,0:T(8,128)(2,1)S(1)} %collective-permute-done.6), channel_id=1, source_target_pairs={{0,2},{1,3},{2,4},{3,5},{4,6},{5,7},{6,0},{7,1},{32,38},{33,39},{3... | collective-permute-start | bytes 786440 | tf_op jit(solution)/shard_map/ppermute | solution.py:26
  81.6 11.4 %collective-permute-start.10 = (bf16[16,16,512]{2,1,0:T(8,128)(2,1)S(1)}, bf16[16,16,512]{2,1,0:T(8,128)(2,1)S(1)}, u32[]{:S(2)}, u32[]{:S(2)}) collective-permute-start(bf16[16,16,512]{2,1,0:T(8,128)(2,1)S(1)} %collective-permute-done.7), channel_id=1, source_target_pairs={{0,7},{1,0},{2,1},{3,2},{4,3},{5,4},{6,5},{7,6},{32,33},{33,34},{3... | collective-permute-start | bytes 786440 | tf_op jit(solution)/shard_map/ppermute | solution.py:26
